TPU v7x, 32 devices: a whole 2x2x4 slice. The times are simulated.
32 devices in a mesh: heads: 4 (over x, core), ctx: 8 (over z, y).
Axes of the slice: x: 2, y: 2, z: 4, core: 2. Of those that a mesh axis runs over, the one named last changes fastest.
Arguments:
- queries: bfloat16 [1536, 2048], P('ctx', 'heads'), may hold values from -6 to 6
- key_states: bfloat16 [1536, 512], P('ctx', 'heads'), may hold values from -6 to 6
- value_states: bfloat16 [1536, 512], P('ctx', 'heads'), may hold values from -6 to 6
- attention_out: bfloat16 [1536, 2048], P('ctx', 'heads'), may hold values from -2 to 2
- out_grad: bfloat16 [1536, 2048], P('ctx', 'heads'), may hold values from -6 to 6
- log_sum_exp: float32 [16, 1536], P('heads', 'ctx'), may hold values from 0 to 16, as said below
- block_counts: int32 [8], replicated, may hold values from 1 to 3, as said below
- w_query: bfloat16 [4096, 2048], P(None, 'heads'), may hold values from -0.09375 to 0.09375
- w_key: bfloat16 [4096, 512], P(None, 'heads'), may hold values from -0.09375 to 0.09375
- w_value: bfloat16 [4096, 512], P(None, 'heads'), may hold values from -0.09375 to 0.09375
Outputs:
- input_grad: bfloat16 [1536, 4096], P('ctx', 'heads')
- key_grad: float32 [1536, 512], P('ctx', 'heads')
- value_grad: float32 [1536, 512], P('ctx', 'heads')
Inputs may be any that keep to these rules, and one draw needn't show every extreme that they name: `block_counts`: one entry equals 3. `log_sum_exp`: finite offsets of each row's scores.
All inputs are finite; a program needn't handle non-finite values.
Results may differ from a plain program's by a relative error of at most 0.0063.
Values may be sent and summed in bfloat16 or wider, within the bound.
A program may use at most 128 MiB of HBM per device.

v0:
```python
import math
import jax
import jax.numpy as jnp
from jax import lax
from jax.sharding import PartitionSpec as P

BLOCK = 64


def key_span(row_count, capacity):
    shards = row_count // capacity
    per_step = max(1, min(shards, 512 // capacity))
    while shards % per_step:
        per_step = per_step - 1
    return per_step * capacity


def row_info(row_index, lengths, offsets, capacity):
    device = row_index // capacity
    onehot = device[:, None] == jnp.arange(lengths.shape[0], dtype=jnp.int32)[None, :]
    length = jnp.sum(jnp.where(onehot, lengths[None, :], 0), axis=1)
    offset = jnp.sum(jnp.where(onehot, offsets[None, :], 0), axis=1)
    within = row_index - device * capacity
    return (offset + within, within < length)


def tile_grads(
    query_blk,
    grad_blk,
    norm_blk,
    delta_blk,
    query_pos,
    query_live,
    key_blk,
    value_blk,
    key_pos,
    key_live,
    score_scale,
):
    scores = (
        jnp.einsum("qgd,kd->gqk", query_blk, key_blk, preferred_element_type=jnp.float32)
        * score_scale
    )
    visible = query_live[:, None] & key_live[None, :] & (key_pos[None, :] <= query_pos[:, None])
    probability = jnp.where(visible[None], jnp.exp(scores - norm_blk.T[:, :, None]), 0.0)
    prob_grad = jnp.einsum("qgd,kd->gqk", grad_blk, value_blk, preferred_element_type=jnp.float32)
    score_grad = probability * (prob_grad - delta_blk.T[:, :, None])
    return (probability.astype(jnp.bfloat16), score_grad.astype(jnp.bfloat16))


def on_device(
    queries,
    key_states,
    value_states,
    attention_out,
    out_grad,
    log_sum_exp,
    block_counts,
    w_query,
    w_key,
    w_value,
):
    capacity = key_states.shape[0]
    head_dim = key_states.shape[1]
    group = queries.shape[1] // head_dim
    score_scale = 1.0 / math.sqrt(head_dim)
    own_index = lax.axis_index("ctx")
    lengths = block_counts * BLOCK
    offsets = jnp.cumsum(lengths) - lengths
    own_rows = own_index * capacity + jnp.arange(capacity, dtype=jnp.int32)
    own_pos, own_live = row_info(own_rows, lengths, offsets, capacity)
    query_heads = queries.reshape(capacity, group, head_dim)
    grad_heads = out_grad.reshape(capacity, group, head_dim)
    output_heads = attention_out.reshape(capacity, group, head_dim)
    delta_rows = jnp.sum(grad_heads.astype(jnp.float32) * output_heads.astype(jnp.float32), axis=2)
    norm_rows = log_sum_exp.T
    zero_rows = jnp.zeros((capacity, group, head_dim), jnp.float32)
    zero_own = jnp.zeros((capacity, head_dim), jnp.float32)
    key_piece = lax.all_gather(key_states, "ctx", axis=0, tiled=True)
    value_piece = lax.all_gather(value_states, "ctx", axis=0, tiled=True)
    span = key_span(key_piece.shape[0], capacity)

    def step(block_num, query_grad):
        begin_row = block_num * span
        key_blk = lax.dynamic_slice_in_dim(key_piece, begin_row, span, 0)
        value_blk = lax.dynamic_slice_in_dim(value_piece, begin_row, span, 0)
        key_pos, key_live = row_info(
            begin_row + jnp.arange(span, dtype=jnp.int32), lengths, offsets, capacity
        )

        def compute():
            prob_b, grad_b = tile_grads(
                query_heads,
                grad_heads,
                norm_rows,
                delta_rows,
                own_pos,
                own_live,
                key_blk,
                value_blk,
                key_pos,
                key_live,
                score_scale,
            )
            return score_scale * jnp.einsum(
                "gqk,kd->qgd", grad_b, key_blk, preferred_element_type=jnp.float32
            )

        terms = compute()
        return query_grad + terms

    query_grad = lax.fori_loop(0, key_piece.shape[0] // span, step, zero_rows)
    norm_all, delta_all = (
        lax.all_gather(norm_rows, "ctx", axis=0, tiled=True),
        lax.all_gather(delta_rows, "ctx", axis=0, tiled=True),
    )
    query_piece = lax.all_gather(queries, "ctx", axis=0, tiled=True)
    grad_piece = lax.all_gather(out_grad, "ctx", axis=0, tiled=True)
    fold_span = key_span(query_piece.shape[0], capacity)

    def step(block_num, state):
        key_acc, value_acc = state
        begin_row = block_num * fold_span
        query_blk = lax.dynamic_slice_in_dim(query_piece, begin_row, fold_span, 0).reshape(
            fold_span, group, head_dim
        )
        grad_blk = lax.dynamic_slice_in_dim(grad_piece, begin_row, fold_span, 0).reshape(
            fold_span, group, head_dim
        )
        norm_blk = lax.dynamic_slice_in_dim(norm_all, begin_row, fold_span, 0)
        delta_blk = lax.dynamic_slice_in_dim(delta_all, begin_row, fold_span, 0)
        query_pos, query_live = row_info(
            begin_row + jnp.arange(fold_span, dtype=jnp.int32), lengths, offsets, capacity
        )

        def compute():
            prob_b, grad_b = tile_grads(
                query_blk,
                grad_blk,
                norm_blk,
                delta_blk,
                query_pos,
                query_live,
                key_states,
                value_states,
                own_pos,
                own_live,
                score_scale,
            )
            return (
                score_scale
                * jnp.einsum("gqk,qgd->kd", grad_b, query_blk, preferred_element_type=jnp.float32),
                jnp.einsum("gqk,qgd->kd", prob_b, grad_blk, preferred_element_type=jnp.float32),
            )

        terms = compute()
        return (key_acc + terms[0], value_acc + terms[1])

    key_grad, value_grad = lax.fori_loop(
        0, query_piece.shape[0] // fold_span, step, (zero_own, zero_own)
    )
    query_flat = query_grad.reshape(capacity, group * head_dim).astype(jnp.bfloat16)
    partial_input = jnp.einsum("rc,mc->rm", query_flat, w_query, preferred_element_type=jnp.float32)
    partial_input = partial_input + jnp.einsum(
        "rc,mc->rm", key_grad.astype(jnp.bfloat16), w_key, preferred_element_type=jnp.float32
    )
    partial_input = partial_input + jnp.einsum(
        "rc,mc->rm", value_grad.astype(jnp.bfloat16), w_value, preferred_element_type=jnp.float32
    )
    input_part = lax.psum_scatter(partial_input, "heads", scatter_dimension=1, tiled=True)
    return (input_part.astype(jnp.bfloat16), key_grad, value_grad)


def solution(mesh):
    return jax.shard_map(
        on_device,
        mesh=mesh,
        in_specs=(
            P("ctx", "heads"),
            P("ctx", "heads"),
            P("ctx", "heads"),
            P("ctx", "heads"),
            P("ctx", "heads"),
            P("heads", "ctx"),
            P(),
            P(None, "heads"),
            P(None, "heads"),
            P(None, "heads"),
        ),
        out_specs=(P("ctx", "heads"), P("ctx", "heads"), P("ctx", "heads")),
        check_vma=False,
    )
```

profile of v0, /device:TPU:0, one launch (start us, length us, event | category | flops | bytes accessed | tf_op | source)
XLA Modules:
  0.0 253.6 jit_solution(5064324992087366843)
XLA Ops:
  15.1 34.2 %all_gather.18 = bf16[1536,128]{1,0:T(8,128)(2,1)S(1)} all-gather(bf16[192,128]{1,0:T(8,128)(2,1)} %param.15), channel_id=1, replica_groups=mesh['heads'=4,'ctx'=8] {'ctx'}, dimensions={0}, use_global_device_ids=true | all-gather | bytes 442368 | tf_op jit(solution)/shard_map/all_gather | solution.py:79
  49.3 33.4 %all_gather.19 = bf16[1536,128]{1,0:T(8,128)(2,1)} all-gather(bf16[192,128]{1,0:T(8,128)(2,1)S(1)} %copy-done.3), channel_id=1, replica_groups=mesh['heads'=4,'ctx'=8] {'ctx'}, dimensions={0}, use_global_device_ids=true | all-gather | bytes 442368 | tf_op jit(solution)/shard_map/all_gather | solution.py:80
  82.7 18.1 %while.34 = (s32[]{:T(128)}, f32[192,4,128]{2,0,1:T(8,128)S(1)}, bf16[1536,128]{1,0:T(8,128)(2,1)S(1)}, pred[192]{0:T(512)(128)(4,1)}, s32[8]{0:T(128)}, /*index...) while((s32[]{:T(128)}, f32[192,4,128]{2,0,1:T(8,128)S(1)}, ...), condition=%wide.region_7.8_spmd.clone, body=%wide.region_4.7_spmd.clone.sunk | while | flops 228805248 | bytes 4005340 | solution.py:112
  84.3 1.4 fusion.93
  85.7 1.5 fusion.94
  88.8 1.4 fusion.93
  90.2 1.5 fusion.94
  93.4 1.4 fusion.93
  94.7 1.5 fusion.94
  97.9 1.4 fusion.93
  99.3 1.5 fusion.94
  100.9 30.6 %all-gather.1 = f32[8,192,4]{1,2,0:T(4,128)S(1)} all-gather(f32[1,192,4]{1,2,0:T(4,128)S(1)} %copy.55), channel_id=1, replica_groups=mesh['heads'=4,'ctx'=8] {'ctx'}, dimensions={0}, use_global_device_ids=true | all-gather | bytes 27648 | tf_op jit(solution)/shard_map/all_gather | solution.py:115
  132.3 30.6 %all-gather = f32[8,192,4]{1,2,0:T(4,128)S(1)} all-gather(f32[1,192,4]{1,2,0:T(4,128)S(1)} %bitcast.173), channel_id=1, replica_groups=mesh['heads'=4,'ctx'=8] {'ctx'}, dimensions={0}, use_global_device_ids=true | all-gather | bytes 27648 | tf_op jit(solution)/shard_map/all_gather | solution.py:114
  163.6 5.4 %fusion.46 = f32[192,4096]{1,0:T(8,128)} fusion(bf16[4096,512]{1,0:T(8,128)(2,1)} %param.21, f32[192,4,128]{2,0,1:T(8,128)S(1)} %get-tuple-element.600), kind=kOutput, calls=%fused_computation.72 | convolution fusion | flops 805404672 | bytes 7733248 | tf_op jit(solution)/shard_map/rc,mc->rm/dot_general | solution.py:163
  168.9 31.9 %while.35 = (s32[]{:T(128)}, f32[192,128]{1,0:T(8,128)S(1)}, f32[192,128]{1,0:T(8,128)}, s32[8]{0:T(128)}, pred[192]{0:T(512)(128)(4,1)}, /*index=5*/s32[192]{0:...) while((s32[]{:T(128)}, f32[192,128]{1,0:T(8,128)S(1)}, ...), condition=%wide.region_11.12_spmd.clone, body=%wide.region_8.11_spmd.clone.sunk | while | flops 304425600 | bytes 8972294 | solution.py:159
  170.5 1.2 constant_dynamic-slice_fusion.3
  171.9 1.3 dynamic-slice_bitcast_fusion.3
  173.2 1.2 fusion.104
  177.8 1.2 constant_dynamic-slice_fusion.3
  179.2 1.3 dynamic-slice_bitcast_fusion.3
  180.5 1.2 fusion.104
  182.0 1.9 fusion.106
  187.4 1.3 dynamic-slice_bitcast_fusion.3
  188.7 1.2 fusion.104
  190.2 1.9 fusion.106
  195.6 1.3 dynamic-slice_bitcast_fusion.3
  196.9 1.2 fusion.104
  198.4 1.9 fusion.106
  200.9 2.6 %convolution_add_fusion.1 = f32[192,4096]{1,0:T(8,128)S(1)} fusion(f32[192,4096]{1,0:T(8,128)} %fusion.46, bf16[4096,128]{1,0:T(8,128)(2,1)S(1)} %copy-done, f32[192,128]{1,0:T(8,128)S(1)} %get-tuple-element.598), kind=kOutput, calls=%fused_computation.70 | convolution fusion | flops 202137600 | bytes 7438336 | tf_op jit(solution)/shard_map/rc,mc->rm/dot_general | solution.py:164
  203.5 2.2 convolution_add_fusion
  205.8 39.4 %reduce-scatter.2.cloned.1.call-done = f32[192,1024]{1,0:T(8,128)} async-done(((f32[192,4096]{1,0:T(8,128)}), f32[192,1024]{1,0:T(8,128)}) %reduce-scatter.2.cloned.1.call-update) | async-done | bytes 786448 | tf_op jit(solution)/shard_map/reduce_scatter | solution.py:170
  245.1 1.9 convert_element_type.61
  (110 shorter events, 29.3 us)
Async XLA Ops:
  7.2 193.7 %copy-start = (bf16[4096,128]{1,0:T(8,128)(2,1)S(1)}, bf16[4096,128]{1,0:T(8,128)(2,1)}, u32[]{:S(2)}) copy-start(bf16[4096,128]{1,0:T(8,128)(2,1)} %param.22) | copy-start | bytes 3145732
  7.2 3.5 %copy-start.5 = (bf16[192,512]{1,0:T(8,128)(2,1)S(1)}, bf16[192,512]{1,0:T(8,128)(2,1)}, u32[]{:S(2)}) copy-start(bf16[192,512]{1,0:T(8,128)(2,1)} %param.14) | copy-start | bytes 589828
  7.2 4.2 %copy-start.9 = (s32[8]{0:T(128)S(1)}, s32[8]{0:T(128)}, u32[]{:S(2)}) copy-start(s32[8]{0:T(128)} %param.20) | copy-start | bytes 100
  7.2 7.4 %copy-start.7 = (bf16[192,512]{1,0:T(8,128)(2,1)S(1)}, bf16[192,512]{1,0:T(8,128)(2,1)}, u32[]{:S(2)}) copy-start(bf16[192,512]{1,0:T(8,128)(2,1)} %param.17) | copy-start | bytes 589828
  7.2 161.7 %all-gather.5.cloned.1.call-start = ((), (), s32[]{:S(2)}) async-start(), calls=%async_computation.1 | async-start | bytes 1769472 | tf_op jit(solution)/shard_map/all_gather | solution.py:117
  7.9 161.0 %all-gather.7.cloned.1.call-start = ((), (), s32[]{:S(2)}) async-start(), calls=%async_computation.2 | async-start | bytes 1769472 | tf_op jit(solution)/shard_map/all_gather | solution.py:118
  8.7 236.4 %reduce-scatter.2.cloned.1.call-start = ((), (), s32[]{:S(2)}) async-start(), calls=%async_computation.3 | async-start | bytes 3932160 | tf_op jit(solution)/shard_map/reduce_scatter | solution.py:170
  10.7 38.6 %copy-start.3 = (bf16[192,128]{1,0:T(8,128)(2,1)S(1)}, bf16[192,128]{1,0:T(8,128)(2,1)}, u32[]{:S(2)}) copy-start(bf16[192,128]{1,0:T(8,128)(2,1)} %param.16) | copy-start | bytes 147460
  11.4 71.3 %copy-start.8 = (f32[4,192]{1,0:T(4,128)S(1)}, f32[4,192]{1,0:T(4,128)}, u32[]{:S(2)}) copy-start(f32[4,192]{1,0:T(4,128)} %param.19) | copy-start | bytes 9220
  174.6 1.0 copy-start.6
  181.9 1.9 copy-start.6
  190.2 1.9 copy-start.6
  198.4 1.9 copy-start.6
  200.9 2.6 %copy-start.1 = (f32[192,128]{1,0:T(8,128)}, f32[192,128]{1,0:T(8,128)S(1)}, u32[]{:S(2)}) copy-start(f32[192,128]{1,0:T(8,128)S(1)} %get-tuple-element.598) | copy-start | bytes 294916
  200.9 2.6 %copy-start.2 = (f32[192,128]{1,0:T(8,128)S(1)}, f32[192,128]{1,0:T(8,128)}, u32[]{:S(2)}) copy-start(f32[192,128]{1,0:T(8,128)} %get-tuple-element.599) | copy-start | bytes 294916
  200.9 2.6 %copy-start.4 = (bf16[4096,128]{1,0:T(8,128)(2,1)S(1)}, bf16[4096,128]{1,0:T(8,128)(2,1)}, u32[]{:S(2)}) copy-start(bf16[4096,128]{1,0:T(8,128)(2,1)} %param.23) | copy-start | bytes 3145732
Sparse Core Ops, SparseCore 0:
  10.2 50.6 all-gather.4
  63.1 43.6 all-gather.6
  205.9 39.1 reduce-scatter.1
where the time goes:
time: 255 us; the launch traced here: 254 us
  blocking collectives  129 us (51%)
  waiting for transfers between devices  40.8 us (16%)
  matrix products  35.5 us (14%)
  other arithmetic  18 us (7%)
  local copies, waits for them, and re-layouts  16 us (6%)
  between operations  13.9 us (5%)
    reduce_scatter x1, waiting for transfers between devices, on_device(): lax.psum_scatter(partial_input, 'heads', scatter_dimension=1, tiled=True)  39.4 us
    all_gather x1, blocking collectives, on_device(): key_piece = lax.all_gather(key_states, 'ctx', axis=0, tiled=True)  34.2 us
    all_gather x1, blocking collectives, on_device(): value_piece = lax.all_gather(value_states, 'ctx', axis=0, tiled=True)  33.4 us
    all_gather x1, blocking collectives, on_device(): lax.all_gather(delta_rows, 'ctx', axis=0, tiled=True)  30.6 us
    all_gather x1, blocking collectives, on_device(): lax.all_gather(norm_rows, 'ctx', axis=0, tiled=True)  30.6 us
    dot_general x8, matrix products, tile_grads(): jnp.einsum('qgd,kd->gqk', query_blk, key_blk, preferred_element_type=jnp....  10.2 us
    dot_general x4, matrix products, compute(): jnp.einsum('gqk,qgd->kd', prob_b, grad_blk, preferred_element_type=jnp.fl...  6.56 us
    and x8, other arithmetic, tile_grads(): query_live[:, None] & key_live[None, :]  6.44 us
  transfers between devices with their start and end apart: 3, of which 1 were waited for; matrix products, arithmetic and copies ran while one was open for 12% of the time, Pallas kernels for 0%

commit v1 on v0

--- a/solution.py
+++ b/solution.py
@@ -76,8 +76,13 @@
     norm_rows = log_sum_exp.T
     zero_rows = jnp.zeros((capacity, group, head_dim), jnp.float32)
     zero_own = jnp.zeros((capacity, head_dim), jnp.float32)
-    key_piece = lax.all_gather(key_states, "ctx", axis=0, tiled=True)
-    value_piece = lax.all_gather(value_states, "ctx", axis=0, tiled=True)
+    key_piece, value_piece = jnp.split(
+        lax.all_gather(
+            jnp.concatenate([key_states, value_states], axis=1), "ctx", axis=0, tiled=True
+        ),
+        [key_states.shape[1]],
+        axis=1,
+    )
     span = key_span(key_piece.shape[0], capacity)
 
     def step(block_num, query_grad):

time: 255 us -> 225 us (0.88)
  blocking collectives: 129 us -> 97.1 us
  matrix products: 35.5 us -> 31 us
  local copies, waits for them, and re-layouts: 16 us -> 19.8 us
  other arithmetic: 18 us -> 21.7 us
    all_gather x2 -> x1, blocking collectives: 67.6 us -> 35.5 us  [on_device(): lax.all_gather(jnp.concatenate([key_states, value_states], axis=1), 'ctx'...]
    dot_general x4, matrix products: 6.56 us -> 1.34 us  [compute(): jnp.einsum('gqk,qgd->kd', prob_b, grad_blk, preferred_element_type=jnp.fl...]
    while x8 -> x40, local copies, waits for them, and re-layouts: 0.02 us -> 3.73 us
  transfers between devices with their start and end apart: 3 -> 3, of which waited for: 1 -> 1; matrix products, arithmetic and copies ran while one was open for 12% -> 14% of each run, Pallas kernels for 0% -> 0%
where the time goes in v1:
time: 225 us; the launch traced here: 224 us
  blocking collectives  97.1 us (43%)
  waiting for transfers between devices  39.9 us (18%)
  matrix products  31 us (14%)
  other arithmetic  21.7 us (10%)
  local copies, waits for them, and re-layouts  19.8 us (9%)
  between operations  13.9 us (6%)
    reduce_scatter x1, waiting for transfers between devices, on_device(): lax.psum_scatter(partial_input, 'heads', scatter_dimension=1, tiled=True)  38.5 us
    all_gather x1, blocking collectives, on_device(): lax.all_gather(jnp.concatenate([key_states, value_states], axis=1), 'ctx'...  35.5 us
    all_gather x1, blocking collectives, on_device(): lax.all_gather(norm_rows, 'ctx', axis=0, tiled=True)  31 us
    all_gather x1, blocking collectives, on_device(): lax.all_gather(delta_rows, 'ctx', axis=0, tiled=True)  30.6 us
    dot_general x8, matrix products, tile_grads(): jnp.einsum('qgd,kd->gqk', query_blk, key_blk, preferred_element_type=jnp....  11 us
    and x8, other arithmetic, tile_grads(): query_live[:, None] & key_live[None, :]  8.93 us
    dot_general x4, matrix products, compute(): jnp.einsum('gqk,kd->qgd', grad_b, key_blk, preferred_element_type=jnp.flo...  6.15 us
    reduce_sum x8, other arithmetic, row_info(): length = jnp.sum(jnp.where(onehot, lengths[None, :], 0), axis=1)  6.11 us
  transfers between devices with their start and end apart: 3, of which 1 were waited for; matrix products, arithmetic and copies ran while one was open for 14% of the time, Pallas kernels for 0%

profile of v1, /device:TPU:0, one launch (start us, length us, event | category | flops | bytes accessed | tf_op | source)
XLA Modules:
  0.0 224.1 jit_solution(4249954665444000589)
XLA Ops:
  8.7 1.6 copy_bitcast_fusion.1
  16.0 35.5 %all_gather.15 = bf16[1536,256]{1,0:T(8,128)(2,1)S(1)} all-gather(bf16[192,256]{1,0:T(8,128)(2,1)S(1)} %pad_maximum_fusion), channel_id=1, replica_groups=mesh['heads'=4,'ctx'=8] {'ctx'}, dimensions={0}, use_global_device_ids=true | all-gather | bytes 884736 | tf_op jit(solution)/shard_map/all_gather | solution.py:80
  52.3 18.5 %while.34 = (s32[]{:T(128)}, f32[192,4,128]{2,0,1:T(8,128)S(1)}, bf16[1536,128]{1,0:T(8,128)(2,1)}, pred[192]{0:T(512)(128)(4,1)}, s32[8]{0:T(128)}, /*index=5*/...) while((s32[]{:T(128)}, f32[192,4,128]{2,0,1:T(8,128)S(1)}, ...), condition=%wide.region_7.8_spmd.clone, body=%wide.region_4.7_spmd.clone.sunk | while | flops 228805248 | bytes 4004324 | solution.py:117
  53.9 1.4 fusion.94
  55.4 1.5 fusion.95
  58.6 1.4 fusion.94
  60.0 1.5 fusion.95
  63.2 1.4 fusion.94
  64.6 1.5 fusion.95
  67.8 1.4 fusion.94
  69.2 1.5 fusion.95
  70.8 31.0 %all-gather = f32[8,192,4]{1,2,0:T(4,128)S(1)} all-gather(f32[1,192,4]{1,2,0:T(4,128)S(1)} %bitcast.173), channel_id=1, replica_groups=mesh['heads'=4,'ctx'=8] {'ctx'}, dimensions={0}, use_global_device_ids=true | all-gather | bytes 27648 | tf_op jit(solution)/shard_map/all_gather | solution.py:119
  102.6 30.6 %all-gather.1 = f32[8,192,4]{1,2,0:T(4,128)S(1)} all-gather(f32[1,192,4]{1,2,0:T(4,128)S(1)} %copy.55), channel_id=1, replica_groups=mesh['heads'=4,'ctx'=8] {'ctx'}, dimensions={0}, use_global_device_ids=true | all-gather | bytes 27648 | tf_op jit(solution)/shard_map/all_gather | solution.py:120
  133.3 5.4 %fusion.46 = f32[192,4096]{1,0:T(8,128)} fusion(bf16[4096,512]{1,0:T(8,128)(2,1)} %param.21, f32[192,4,128]{2,0,1:T(8,128)S(1)} %get-tuple-element.600), kind=kOutput, calls=%fused_computation.72 | convolution fusion | flops 805404672 | bytes 7733248 | tf_op jit(solution)/shard_map/rc,mc->rm/dot_general | solution.py:168
  138.6 33.6 %while.35 = (s32[]{:T(128)}, f32[192,128]{1,0:T(8,128)S(1)}, f32[192,128]{1,0:T(8,128)}, s32[8]{0:T(128)}, pred[192]{0:T(512)(128)(4,1)}, /*index=5*/s32[192]{0:...) while((s32[]{:T(128)}, f32[192,128]{1,0:T(8,128)S(1)}, ...), condition=%wide.region_11.12_spmd.clone, body=%wide.region_8.11_spmd.clone.sunk | while | flops 304425600 | bytes 9955454 | solution.py:164
  139.5 1.3 dynamic-slice_bitcast_fusion.3
  140.8 1.4 compare_and_fusion.5
  143.8 1.3 fusion.105
  147.9 1.3 dynamic-slice_bitcast_fusion.3
  149.2 1.4 compare_and_fusion.5
  150.6 1.2 constant_dynamic-slice_fusion.3
  152.2 1.3 fusion.105
  156.3 1.3 dynamic-slice_bitcast_fusion.3
  157.6 1.4 compare_and_fusion.5
  160.6 1.3 fusion.105
  164.7 1.3 dynamic-slice_bitcast_fusion.3
  166.0 1.4 compare_and_fusion.5
  169.0 1.3 fusion.105
  172.3 2.6 %convolution_add_fusion.1 = f32[192,4096]{1,0:T(8,128)S(1)} fusion(f32[192,4096]{1,0:T(8,128)} %fusion.46, bf16[4096,128]{1,0:T(8,128)(2,1)S(1)} %copy-done, f32[192,128]{1,0:T(8,128)S(1)} %get-tuple-element.598), kind=kOutput, calls=%fused_computation.70 | convolution fusion | flops 202137600 | bytes 7438336 | tf_op jit(solution)/shard_map/rc,mc->rm/dot_general | solution.py:169
  174.9 2.2 convolution_add_fusion
  177.1 38.5 %reduce-scatter.2.cloned.1.call-done = f32[192,1024]{1,0:T(8,128)} async-done(((f32[192,4096]{1,0:T(8,128)}), f32[192,1024]{1,0:T(8,128)}) %reduce-scatter.2.cloned.1.call-update) | async-done | bytes 786448 | tf_op jit(solution)/shard_map/reduce_scatter | solution.py:175
  215.6 1.9 convert_element_type.61
  (143 shorter events, 31.1 us)
Async XLA Ops:
  7.2 165.1 %copy-start = (bf16[4096,128]{1,0:T(8,128)(2,1)S(1)}, bf16[4096,128]{1,0:T(8,128)(2,1)}, u32[]{:S(2)}) copy-start(bf16[4096,128]{1,0:T(8,128)(2,1)} %param.22) | copy-start | bytes 3145732
  7.2 4.2 %copy-start.5 = (bf16[192,512]{1,0:T(8,128)(2,1)S(1)}, bf16[192,512]{1,0:T(8,128)(2,1)}, u32[]{:S(2)}) copy-start(bf16[192,512]{1,0:T(8,128)(2,1)} %param.18) | copy-start | bytes 589828
  7.2 4.3 %copy-start.13 = (s32[8]{0:T(128)S(1)}, s32[8]{0:T(128)}, u32[]{:S(2)}) copy-start(s32[8]{0:T(128)} %param.20) | copy-start | bytes 100
  7.2 7.5 %copy-start.9 = (bf16[192,512]{1,0:T(8,128)(2,1)S(1)}, bf16[192,512]{1,0:T(8,128)(2,1)}, u32[]{:S(2)}) copy-start(bf16[192,512]{1,0:T(8,128)(2,1)} %param.17) | copy-start | bytes 589828
  7.2 131.4 %all-gather.5.cloned.1.call-start = ((), (), s32[]{:S(2)}) async-start(), calls=%async_computation.1 | async-start | bytes 1769472 | tf_op jit(solution)/shard_map/all_gather | solution.py:122
  7.9 130.7 %all-gather.7.cloned.1.call-start = ((), (), s32[]{:S(2)}) async-start(), calls=%async_computation.2 | async-start | bytes 1769472 | tf_op jit(solution)/shard_map/all_gather | solution.py:123
  8.7 206.9 %reduce-scatter.2.cloned.1.call-start = ((), (), s32[]{:S(2)}) async-start(), calls=%async_computation.3 | async-start | bytes 3932160 | tf_op jit(solution)/shard_map/reduce_scatter | solution.py:175
  10.4 4.8 %copy-start.6 = (bf16[192,128]{1,0:T(8,128)(2,1)S(1)}, bf16[192,128]{1,0:T(8,128)(2,1)}, u32[]{:S(2)}) copy-start(bf16[192,128]{1,0:T(8,128)(2,1)} %param.16) | copy-start | bytes 147460
  16.0 36.3 %copy-start.12 = (f32[4,192]{1,0:T(4,128)S(1)}, f32[4,192]{1,0:T(4,128)}, u32[]{:S(2)}) copy-start(f32[4,192]{1,0:T(4,128)} %param.19) | copy-start | bytes 9220
  138.6 4.7 %copy-start.10 = (f32[1536,4]{0,1:T(4,128)}, f32[1536,4]{0,1:T(4,128)S(1)}, u32[]{:S(2)}) copy-start(f32[1536,4]{0,1:T(4,128)S(1)} %get-tuple-element.1085) | copy-start | bytes 73732 | tf_op jit(solution)/shard_map/while
  143.8 1.3 copy-start.8
  145.2 0.9 copy-start.2
  146.1 1.0 copy-start.11
  146.4 0.6 copy-start.3
  147.0 4.7 %copy-start.10 = (f32[1536,4]{0,1:T(4,128)}, f32[1536,4]{0,1:T(4,128)S(1)}, u32[]{:S(2)}) copy-start(f32[1536,4]{0,1:T(4,128)S(1)} %get-tuple-element.1085) | copy-start | bytes 73732 | tf_op jit(solution)/shard_map/while
  152.2 1.3 copy-start.8
  153.6 0.9 copy-start.2
  154.5 1.0 copy-start.11
  154.8 0.6 copy-start.3
  155.5 4.7 %copy-start.10 = (f32[1536,4]{0,1:T(4,128)}, f32[1536,4]{0,1:T(4,128)S(1)}, u32[]{:S(2)}) copy-start(f32[1536,4]{0,1:T(4,128)S(1)} %get-tuple-element.1085) | copy-start | bytes 73732 | tf_op jit(solution)/shard_map/while
  160.6 1.3 copy-start.8
  162.0 0.9 copy-start.2
  162.9 1.0 copy-start.11
  163.2 0.6 copy-start.3
  163.9 4.7 %copy-start.10 = (f32[1536,4]{0,1:T(4,128)}, f32[1536,4]{0,1:T(4,128)S(1)}, u32[]{:S(2)}) copy-start(f32[1536,4]{0,1:T(4,128)S(1)} %get-tuple-element.1085) | copy-start | bytes 73732 | tf_op jit(solution)/shard_map/while
  169.0 1.3 copy-start.8
  170.4 0.9 copy-start.2
  171.3 1.0 copy-start.11
  171.6 0.6 copy-start.3
  172.3 2.6 %copy-start.1 = (f32[192,128]{1,0:T(8,128)}, f32[192,128]{1,0:T(8,128)S(1)}, u32[]{:S(2)}) copy-start(f32[192,128]{1,0:T(8,128)S(1)} %get-tuple-element.598) | copy-start | bytes 294916
  172.3 2.6 %copy-start.4 = (f32[192,128]{1,0:T(8,128)S(1)}, f32[192,128]{1,0:T(8,128)}, u32[]{:S(2)}) copy-start(f32[192,128]{1,0:T(8,128)} %get-tuple-element.599) | copy-start | bytes 294916
  172.3 2.6 %copy-start.7 = (bf16[4096,128]{1,0:T(8,128)(2,1)S(1)}, bf16[4096,128]{1,0:T(8,128)(2,1)}, u32[]{:S(2)}) copy-start(bf16[4096,128]{1,0:T(8,128)(2,1)} %param.23) | copy-start | bytes 3145732
Sparse Core Ops, SparseCore 0:
  10.2 50.9 all-gather.4
  63.4 43.5 all-gather.6
  177.3 38.3 reduce-scatter.1
